TPU v7x, 32 devices: a whole 2x2x4 slice. The times are simulated.
32 devices in a mesh: dp: 4 (over y, x), expert: 8 (over z, core).
Axes of the slice: x: 2, y: 2, z: 4, core: 2. Of those that a mesh axis runs over, the one named last changes fastest.
Arguments:
- hidden: bfloat16 [8, 4608, 1408], P('expert', 'dp')
- upstream: bfloat16 [8, 4608, 2048], P('expert', 'dp')
- token_counts: int32 [8, 4], P('expert', 'dp'), may hold values from 1 to 1152, as said below
- master: float32 [8, 1408, 2048], P('expert', 'dp'), may hold values from -0.15625 to 0.15625
- first_moment: float32 [8, 1408, 2048], P('expert', 'dp'), may hold values from -6 to 6
- second_moment: float32 [8, 1408, 2048], P('expert', 'dp'), may hold values from 0.25 to 4
- router_input: bfloat16 [4096, 2048], P(('dp', 'expert')), may hold values from -6 to 6
- router_cot: bfloat16 [64, 4096], P(None, ('dp', 'expert'))
- router_master: float32 [64, 2048], replicated, may hold values from -0.125 to 0.125
- router_first: float32 [64, 2048], replicated, may hold values from -6 to 6
- router_second: float32 [64, 2048], replicated, may hold values from 0.25 to 4
- partner: int32 [8], replicated, may hold values from 0 to 7, as said below
Outputs:
- new_weight: bfloat16 [8, 1408, 2048], P('expert')
- new_master: float32 [8, 1408, 2048], P('expert', 'dp')
- new_first: float32 [8, 1408, 2048], P('expert', 'dp')
- new_second: float32 [8, 1408, 2048], P('expert', 'dp')
- router_master_new: float32 [64, 2048], replicated
- router_first_new: float32 [64, 2048], replicated
- router_second_new: float32 [64, 2048], replicated
Inputs may be any that keep to these rules, and one draw needn't show every extreme that they name: partner[partner[p]] = p for every position p; a position with partner[p] = p keeps its expert. The first token_counts[e, d] of replica d's 1152 slots for position e are live, the rest are padding.
All inputs are finite; a program needn't handle non-finite values.
Results may differ from a plain program's by a relative error of at most 0.001.
Values may be sent and summed in bfloat16 or wider, within the bound.
A program may use at most 128 MiB of HBM per device.

v0:
```python
import math
import jax
import jax.numpy as jnp
from jax import lax
from jax.sharding import PartitionSpec as P

beta_first = 0.9
beta_second = 0.95
learn_rate = 0.001
decay_weight = 0.1
adam_eps = 1e-08
norm_eps = 1e-06
correct_first = 1.0 - 0.9**10
correct_second = 1.0 - 0.95**10


def adam_update(gradient, moment_one, moment_two, weights):
    first_new = beta_first * moment_one + (1.0 - beta_first) * gradient
    second_new = beta_second * moment_two + (1.0 - beta_second) * gradient * gradient
    ratio = first_new / correct_first / (jnp.sqrt(second_new / correct_second) + adam_eps)
    weights_new = weights - learn_rate * (ratio + decay_weight * weights)
    return (weights_new, first_new, second_new)


def split_pieces(matrix, groups):
    return matrix.reshape(matrix.shape[0], groups, matrix.shape[1] // groups)


def relocate_state(states, partner):
    groups = lax.axis_size("expert")
    pieces = tuple((split_pieces(member, groups) for member in states))

    def reorder(received):
        arranged = tuple((jnp.take(member, partner, axis=1) for member in received))
        return lax.all_to_all(arranged, "expert", split_axis=1, concat_axis=1, tiled=True)

    result = reorder(
        (
            lax.all_to_all(pieces[0], "expert", split_axis=1, concat_axis=1, tiled=True),
            lax.all_to_all(pieces[1], "expert", split_axis=1, concat_axis=1, tiled=True),
            lax.all_to_all(pieces[2], "expert", split_axis=1, concat_axis=1, tiled=True),
        )
    )
    return tuple((member.reshape(member.shape[0], -1) for member in result))


def regather(weight_shard):
    return lax.all_gather(weight_shard, "dp", axis=0, tiled=True)


def on_device(
    hidden,
    upstream,
    token_counts,
    master,
    first_moment,
    second_moment,
    router_input,
    router_cot,
    router_master,
    router_first,
    router_second,
    partner,
):
    hidden_units = hidden.shape[2]
    features = upstream.shape[2]
    row_count = hidden.shape[1]
    live_rows = jnp.arange(row_count, dtype=jnp.int32) < token_counts[0, 0]
    activations = hidden[0]
    grads_out = upstream[0]
    masked_out = jnp.where(live_rows[:, None], grads_out, jnp.zeros_like(grads_out))
    router_partial = jnp.dot(router_cot, router_input, preferred_element_type=jnp.float32)
    gradient = lax.psum_scatter(
        lax.dot_general(
            activations, masked_out, (((0,), (0,)), ((), ())), preferred_element_type=jnp.float32
        ),
        "dp",
        scatter_dimension=0,
        tiled=True,
    )
    router_grad, expert_square = lax.psum(
        (router_partial, jnp.sum(gradient * gradient)), ("dp", "expert")
    )
    total_square = expert_square + jnp.sum(router_grad * router_grad)
    clip_limit = 2.0 * math.sqrt(
        float(lax.axis_size("expert") * hidden_units * features + router_cot.shape[0] * features)
    )
    factor = jnp.minimum(1.0, clip_limit / (jnp.sqrt(total_square) + norm_eps))
    master_new, first_new, second_new = adam_update(
        factor * gradient, first_moment[0], second_moment[0], master[0]
    )
    router_outs = adam_update(factor * router_grad, router_first, router_second, router_master)
    moved = relocate_state((master_new, first_new, second_new), partner)
    moved_weight = regather(moved[0].astype(jnp.bfloat16))
    return (
        moved_weight[None],
        moved[0][None],
        moved[1][None],
        moved[2][None],
        router_outs[0],
        router_outs[1],
        router_outs[2],
    )


def solution(mesh):
    in_specs = (
        P("expert", "dp", None),
        P("expert", "dp", None),
        P("expert", "dp"),
        P("expert", "dp", None),
        P("expert", "dp", None),
        P("expert", "dp", None),
        P(("dp", "expert"), None),
        P(None, ("dp", "expert")),
        P(),
        P(),
        P(),
        P(),
    )
    out_specs = (
        P("expert", None, None),
        P("expert", "dp", None),
        P("expert", "dp", None),
        P("expert", "dp", None),
        P(),
        P(),
        P(),
    )
    return jax.shard_map(
        on_device, mesh=mesh, in_specs=in_specs, out_specs=out_specs, check_vma=False
    )
```

profile of v0, /device:TPU:0, one launch (start us, length us, event | category | flops | bytes accessed | tf_op | source)
XLA Modules:
  0.0 716.0 jit_solution(1665810783923439618)
XLA Ops:
  9.9 12.9 %convolution_bitcast_fusion = f32[1408,2048]{0,1:T(8,128)} fusion(bf16[1,1152,2048]{2,1,0:T(8,128)(2,1)} %param.15, pred[1152]{0:T(1024)(128)(4,1)S(1)} %iota_compare_fusion, bf16[1,1152,1408]{2,1,0:T(8,128)(2,1)S(1)} %copy-done), kind=kOutput, calls=%fused_computation.3 | convolution fusion | flops 6646136832 | bytes 19498112 | tf_op jit(solution)/shard_map/dot_general | solution.py:74
  22.8 12.0 %copy.42 = f32[1408,2048]{1,0:T(8,128)} copy(f32[1408,2048]{0,1:T(8,128)} %convolution_bitcast_fusion) | data formatting | bytes 23068672
  37.8 2.3 copy.32
  40.1 3.6 copy.33
  43.8 2.4 copy.34
  46.2 105.0 %reduce-scatter.4.cloned.1.call-done = f32[352,2048]{1,0:T(8,128)} async-done(((f32[1408,2048]{1,0:T(8,128)}), f32[352,2048]{1,0:T(8,128)}) %reduce-scatter.4.cloned.1.call-update) | async-done | bytes 2883600
  151.1 2.3 copy.43
  154.9 58.7 %all-reduce.2.cloned.1.call-done = f32[64,2048]{1,0:T(8,128)} async-done(((f32[64,2048]{1,0:T(8,128)}), f32[64,2048]{1,0:T(8,128)}) %all-reduce.2.cloned.1.call-update) | async-done | bytes 524304 | tf_op jit(solution)/shard_map/psum | solution.py:81
  215.4 39.5 %psum.14 = f32[]{:T(128)} all-reduce(f32[]{:T(128)} %multiply_reduce_fusion), channel_id=1, replica_groups=mesh['dp'=4,'expert'=8] {'dp','expert'}, use_global_device_ids=true, to_apply=%region_2.3 | all-reduce | flops 1 | bytes 8 | tf_op jit(solution)/shard_map/psum | solution.py:81
  256.2 6.9 bitcast_subtract_fusion
  263.1 3.4 copy.35
  266.6 4.7 all-to-all-start
  273.5 63.6 %all-to-all-done = f32[352,8,256]{2,0,1:T(8,128)} async-done(((f32[352,8,256]{2,0,1:T(8,128)}), f32[352,8,256]{2,0,1:T(8,128)}, u32[]{:S(2)}, u32[]{:S(2)}) %all-to-all-start) | async-done | bytes 2883616 | tf_op jit(solution)/shard_map/all_to_all | solution.py:39
  337.1 4.4 all-to-all-start.2
  343.9 63.6 %all-to-all-done.2 = f32[352,8,256]{2,0,1:T(8,128)} async-done(((f32[352,8,256]{2,0,1:T(8,128)}), f32[352,8,256]{2,0,1:T(8,128)}, u32[]{:S(2)}, u32[]{:S(2)}) %all-to-all-start.2) | async-done | bytes 2883616 | tf_op jit(solution)/shard_map/all_to_all | solution.py:40
  407.5 4.6 all-to-all-start.4
  412.1 2.5 gather_fusion
  414.7 4.1 gather_fusion.1
  418.8 59.0 %all-to-all-done.4 = f32[352,8,256]{2,0,1:T(8,128)} async-done(((f32[352,8,256]{2,0,1:T(8,128)}), f32[352,8,256]{2,0,1:T(8,128)}, u32[]{:S(2)}, u32[]{:S(2)}) %all-to-all-start.4) | async-done | bytes 2883616 | tf_op jit(solution)/shard_map/all_to_all | solution.py:41
  477.8 4.1 gather_fusion.2
  481.9 6.0 select_bitcast_fusion
  487.9 68.3 %all_to_all.30 = f32[352,8,256]{2,0,1:T(8,128)S(1)} all-to-all(f32[352,8,256]{2,0,1:T(8,128)S(1)} %get-tuple-element.16), channel_id=1, replica_groups=mesh['dp'=4,'expert'=8] {'expert'}, dimensions={1} | all-to-all | bytes 5767168 | tf_op jit(solution)/shard_map/all_to_all | solution.py:35
  556.3 4.4 all-to-all-start.3
  562.2 64.4 %all-to-all-done.3 = f32[352,8,256]{2,0,1:T(8,128)} async-done(((f32[352,8,256]{2,0,1:T(8,128)}), f32[352,8,256]{2,0,1:T(8,128)}, u32[]{:S(2)}, u32[]{:S(2)}) %all-to-all-start.3) | async-done | bytes 2883616 | tf_op jit(solution)/shard_map/all_to_all | solution.py:35
  626.6 4.5 all-to-all-start.5
  631.1 2.9 multiply_subtract_fusion
  634.0 3.2 copy.37
  637.2 4.2 broadcast_in_dim_reshape.9
  641.4 3.5 copy.39
  646.7 50.3 %all-to-all-done.5 = f32[352,8,256]{2,0,1:T(8,128)} async-done(((f32[352,8,256]{2,0,1:T(8,128)}), f32[352,8,256]{2,0,1:T(8,128)}, u32[]{:S(2)}, u32[]{:S(2)}) %all-to-all-start.5) | async-done | bytes 2883616 | tf_op jit(solution)/shard_map/all_to_all | solution.py:35
  696.9 3.5 copy.41
  702.2 6.3 copy.48
  (36 shorter events, 16.9 us)
Async XLA Ops:
  8.0 1.9 copy-start
  8.0 143.1 %reduce-scatter.4.cloned.1.call-start = ((), (), s32[]{:S(2)}) async-start(), calls=%async_computation.9 | async-start | bytes 14417920
  34.8 0.7 copy-start.6
  34.8 3.0 copy-start.4
  34.8 178.7 %all-reduce.2.cloned.1.call-start = ((), (), s32[]{:S(2)}) async-start(), calls=%async_computation.7 | async-start | bytes 1048576 | tf_op jit(solution)/shard_map/psum | solution.py:81
  40.1 3.6 copy-start.5
  266.6 4.7 copy-start.3
  266.6 70.6 %all-to-all-start = ((f32[352,8,256]{2,0,1:T(8,128)}), f32[352,8,256]{2,0,1:T(8,128)}, u32[]{:S(2)}, u32[]{:S(2)}) async-start(f32[352,8,256]{2,0,1:T(8,128)} %copy.35), calls=%async_computation | async-start | bytes 5767168 | tf_op jit(solution)/shard_map/all_to_all | solution.py:39
  273.5 68.1 %copy-start.2 = (f32[352,2048]{0,1:T(8,128)S(1)}, f32[352,2048]{0,1:T(8,128)}, u32[]{:S(2)}) copy-start(f32[352,2048]{0,1:T(8,128)} %get-tuple-element.13) | copy-start | bytes 8650756
  337.1 70.3 %all-to-all-start.2 = ((f32[352,8,256]{2,0,1:T(8,128)}), f32[352,8,256]{2,0,1:T(8,128)}, u32[]{:S(2)}, u32[]{:S(2)}) async-start(f32[352,8,256]{2,0,1:T(8,128)} %copy.38), calls=%async_computation.2 | async-start | bytes 5767168 | tf_op jit(solution)/shard_map/all_to_all | solution.py:40
  343.9 68.2 %copy-start.7 = (s32[8]{0:T(128)S(1)}, s32[8]{0:T(128)}, u32[]{:S(2)}) copy-start(s32[8]{0:T(128)} %param.25) | copy-start | bytes 100
  407.5 70.3 %all-to-all-start.4 = ((f32[352,8,256]{2,0,1:T(8,128)}), f32[352,8,256]{2,0,1:T(8,128)}, u32[]{:S(2)}, u32[]{:S(2)}) async-start(f32[352,8,256]{2,0,1:T(8,128)} %copy.40), calls=%async_computation.4 | async-start | bytes 5767168 | tf_op jit(solution)/shard_map/all_to_all | solution.py:41
  556.3 70.3 %all-to-all-start.3 = ((f32[352,8,256]{2,0,1:T(8,128)}), f32[352,8,256]{2,0,1:T(8,128)}, u32[]{:S(2)}, u32[]{:S(2)}) async-start(f32[352,8,256]{2,0,1:T(8,128)} %get-tuple-element.15), calls=%async_computation.3 | async-start | bytes 5767168 | tf_op jit(solution)/shard_map/all_to_all | solution.py:35
  560.7 141.6 %all-gather.2.cloned.1.call-start = ((), (), s32[]{:S(2)}) async-start(), calls=%async_computation.8 | async-start | bytes 7208960 | tf_op jit(solution)/shard_map/all_gather | solution.py:48
  626.6 70.4 %all-to-all-start.5 = ((f32[352,8,256]{2,0,1:T(8,128)}), f32[352,8,256]{2,0,1:T(8,128)}, u32[]{:S(2)}, u32[]{:S(2)}) async-start(f32[352,8,256]{2,0,1:T(8,128)} %get-tuple-element.14), calls=%async_computation.5 | async-start | bytes 5767168 | tf_op jit(solution)/shard_map/all_to_all | solution.py:35
  702.2 6.3 copy-start.1
Sparse Core Ops, SparseCore 0:
  35.0 116.1 reduce-scatter.3
  563.9 67.7 all-gather.1
Sparse Core Ops, SparseCore 1:
  41.2 172.3 all-reduce.1
where the time goes:
time: 717 us; the launch traced here: 716 us
  waiting for transfers between devices  465 us (65%)
  blocking collectives  108 us (15%)
  local copies, waits for them, and re-layouts  68.8 us (10%)
  starting transfers between devices  22.7 us (3%)
  other arithmetic  19.2 us (3%)
  between operations  17.8 us (2%)
  matrix products  15.1 us (2%)
    all_to_all x2, waiting for transfers between devices, reorder(): lax.all_to_all(arranged, 'expert', split_axis=1, concat_axis=1, tiled=True)  115 us
    unnamed x4, waiting for transfers between devices  105 us
    all_to_all x1, blocking collectives, reorder(): lax.all_to_all(arranged, 'expert', split_axis=1, concat_axis=1, tiled=True)  68.3 us
    all_to_all x1, waiting for transfers between devices, relocate_state(): lax.all_to_all(pieces[1], 'expert', split_axis=1, concat_axis=1, tiled=True)  63.6 us
    all_to_all x1, waiting for transfers between devices, relocate_state(): lax.all_to_all(pieces[0], 'expert', split_axis=1, concat_axis=1, tiled=True)  63.6 us
    all_to_all x1, waiting for transfers between devices, relocate_state(): lax.all_to_all(pieces[2], 'expert', split_axis=1, concat_axis=1, tiled=True)  59 us
    psum x1, waiting for transfers between devices, on_device(): lax.psum((router_partial, jnp.sum(gradient * gradient)), ('dp', 'expert'))  58.7 us
    psum x1, blocking collectives, on_device(): lax.psum((router_partial, jnp.sum(gradient * gradient)), ('dp', 'expert'))  39.5 us
  transfers between devices with their start and end apart: 8, of which 7 were waited for; matrix products, arithmetic and copies ran while one was open for 7% of the time, Pallas kernels for 0%

commit v1 on v0

--- a/solution.py
+++ b/solution.py
@@ -38,7 +38,12 @@
         (
             lax.all_to_all(pieces[0], "expert", split_axis=1, concat_axis=1, tiled=True),
             lax.all_to_all(pieces[1], "expert", split_axis=1, concat_axis=1, tiled=True),
-            lax.all_to_all(pieces[2], "expert", split_axis=1, concat_axis=1, tiled=True),
+            jnp.concatenate(
+                lax.all_to_all(
+                    jnp.stack(jnp.split(pieces[2], lax.axis_size("expert"), axis=1)), "expert", 0, 0
+                ),
+                axis=1,
+            ),
         )
     )
     return tuple((member.reshape(member.shape[0], -1) for member in result))

time: 717 us -> 734 us (1.024)
  local copies, waits for them, and re-layouts: 68.8 us -> 82.6 us
    unnamed x22 -> x37, local copies, waits for them, and re-layouts: 30.8 us -> 39 us
  transfers between devices with their start and end apart: 8 -> 8, of which waited for: 7 -> 7; matrix products, arithmetic and copies ran while one was open for 7% -> 8% of each run, Pallas kernels for 0% -> 0%
where the time goes in v1:
time: 734 us; the launch traced here: 733 us
  waiting for transfers between devices  468 us (64%)
  blocking collectives  108 us (15%)
  local copies, waits for them, and re-layouts  82.6 us (11%)
  starting transfers between devices  22.7 us (3%)
  other arithmetic  18.9 us (3%)
  between operations  17.9 us (2%)
  matrix products  15.1 us (2%)
    all_to_all x2, waiting for transfers between devices, reorder(): lax.all_to_all(arranged, 'expert', split_axis=1, concat_axis=1, tiled=True)  118 us
    unnamed x4, waiting for transfers between devices  105 us
    all_to_all x1, blocking collectives, reorder(): lax.all_to_all(arranged, 'expert', split_axis=1, concat_axis=1, tiled=True)  68.3 us
    all_to_all x1, waiting for transfers between devices, relocate_state(): lax.all_to_all(jnp.stack(jnp.split(pieces[2], lax.axis_size('expert'), ax...  63.6 us
    all_to_all x1, waiting for transfers between devices, relocate_state(): lax.all_to_all(pieces[0], 'expert', split_axis=1, concat_axis=1, tiled=True)  63.4 us
    all_to_all x1, waiting for transfers between devices, relocate_state(): lax.all_to_all(pieces[1], 'expert', split_axis=1, concat_axis=1, tiled=True)  59.2 us
    psum x1, waiting for transfers between devices, on_device(): lax.psum((router_partial, jnp.sum(gradient * gradient)), ('dp', 'expert'))  58.7 us
    psum x1, blocking collectives, on_device(): lax.psum((router_partial, jnp.sum(gradient * gradient)), ('dp', 'expert'))  39.5 us
  transfers between devices with their start and end apart: 8, of which 7 were waited for; matrix products, arithmetic and copies ran while one was open for 8% of the time, Pallas kernels for 0%

profile of v1, /device:TPU:0, one launch (start us, length us, event | category | flops | bytes accessed | tf_op | source)
XLA Modules:
  0.0 733.0 jit_solution(525391761075048116)
XLA Ops:
  9.9 12.9 %convolution_bitcast_fusion = f32[1408,2048]{0,1:T(8,128)} fusion(bf16[1,1152,2048]{2,1,0:T(8,128)(2,1)} %param.15, pred[1152]{0:T(1024)(128)(4,1)S(1)} %iota_compare_fusion, bf16[1,1152,1408]{2,1,0:T(8,128)(2,1)S(1)} %copy-done), kind=kOutput, calls=%fused_computation.3 | convolution fusion | flops 6646136832 | bytes 19498112 | tf_op jit(solution)/shard_map/dot_general | solution.py:79
  22.8 12.0 %copy.56 = f32[1408,2048]{1,0:T(8,128)} copy(f32[1408,2048]{0,1:T(8,128)} %convolution_bitcast_fusion) | data formatting | bytes 23068672
  37.8 2.3 copy.39
  40.1 3.6 copy.40
  43.8 2.4 copy.41
  46.2 105.0 %reduce-scatter.4.cloned.1.call-done = f32[352,2048]{1,0:T(8,128)} async-done(((f32[1408,2048]{1,0:T(8,128)}), f32[352,2048]{1,0:T(8,128)}) %reduce-scatter.4.cloned.1.call-update) | async-done | bytes 2883600
  154.9 58.7 %all-reduce.2.cloned.1.call-done = f32[64,2048]{1,0:T(8,128)} async-done(((f32[64,2048]{1,0:T(8,128)}), f32[64,2048]{1,0:T(8,128)}) %all-reduce.2.cloned.1.call-update) | async-done | bytes 524304 | tf_op jit(solution)/shard_map/psum | solution.py:86
  215.4 39.5 %psum.14 = f32[]{:T(128)} all-reduce(f32[]{:T(128)} %multiply_reduce_fusion), channel_id=1, replica_groups=mesh['dp'=4,'expert'=8] {'dp','expert'}, use_global_device_ids=true, to_apply=%region_2.3 | all-reduce | flops 1 | bytes 8 | tf_op jit(solution)/shard_map/psum | solution.py:86
  256.2 6.6 bitcast_subtract_fusion
  272.2 4.7 all-to-all-start.4
  279.2 63.6 %all-to-all-done.4 = f32[8,352,1,256]{3,1,2,0:T(8,128)} async-done(((f32[8,352,1,256]{3,1,2,0:T(8,128)}), f32[8,352,1,256]{3,1,2,0:T(8,128)}, u32[]{:S(2)}, u32[]{:S(2)}) %all-to-all-start.4) | async-done | bytes 2883616 | tf_op jit(solution)/shard_map/all_to_all | solution.py:42
  342.8 4.6 all-to-all-start
  349.7 63.4 %all-to-all-done = f32[352,8,256]{2,0,1:T(8,128)} async-done(((f32[352,8,256]{2,0,1:T(8,128)}), f32[352,8,256]{2,0,1:T(8,128)}, u32[]{:S(2)}, u32[]{:S(2)}) %all-to-all-start) | async-done | bytes 2883616 | tf_op jit(solution)/shard_map/all_to_all | solution.py:39
  413.1 4.4 all-to-all-start.2
  417.6 2.5 gather_fusion.2
  420.1 4.1 gather_fusion
  424.3 59.2 %all-to-all-done.2 = f32[352,8,256]{2,0,1:T(8,128)} async-done(((f32[352,8,256]{2,0,1:T(8,128)}), f32[352,8,256]{2,0,1:T(8,128)}, u32[]{:S(2)}, u32[]{:S(2)}) %all-to-all-start.2) | async-done | bytes 2883616 | tf_op jit(solution)/shard_map/all_to_all | solution.py:40
  483.4 4.1 gather_fusion.1
  487.5 6.0 select_bitcast_fusion
  493.6 68.3 %all_to_all.30 = f32[352,8,256]{2,0,1:T(8,128)S(1)} all-to-all(f32[352,8,256]{2,0,1:T(8,128)S(1)} %get-tuple-element.24), channel_id=1, replica_groups=mesh['dp'=4,'expert'=8] {'expert'}, dimensions={1} | all-to-all | bytes 5767168 | tf_op jit(solution)/shard_map/all_to_all | solution.py:35
  561.9 4.4 all-to-all-start.3
  567.9 64.3 %all-to-all-done.3 = f32[352,8,256]{2,0,1:T(8,128)} async-done(((f32[352,8,256]{2,0,1:T(8,128)}), f32[352,8,256]{2,0,1:T(8,128)}, u32[]{:S(2)}, u32[]{:S(2)}) %all-to-all-start.3) | async-done | bytes 2883616 | tf_op jit(solution)/shard_map/all_to_all | solution.py:35
  632.2 4.5 all-to-all-start.5
  636.7 2.9 multiply_subtract_fusion
  639.6 5.1 copy.46
  644.7 4.2 broadcast_in_dim_reshape.10
  648.9 53.7 %all-to-all-done.5 = f32[352,8,256]{2,0,1:T(8,128)} async-done(((f32[352,8,256]{2,0,1:T(8,128)}), f32[352,8,256]{2,0,1:T(8,128)}, u32[]{:S(2)}, u32[]{:S(2)}) %all-to-all-start.5) | async-done | bytes 2883616 | tf_op jit(solution)/shard_map/all_to_all | solution.py:35
  702.6 5.1 copy.55
  707.7 4.2 broadcast_in_dim_reshape.11
  711.8 3.2 copy.44
  715.1 4.2 broadcast_in_dim_reshape.9
  719.3 6.3 copy.77
  (52 shorter events, 25.0 us)
Async XLA Ops:
  8.0 1.9 copy-start
  8.0 143.1 %reduce-scatter.4.cloned.1.call-start = ((), (), s32[]{:S(2)}) async-start(), calls=%async_computation.9 | async-start | bytes 14417920
  34.8 0.7 copy-start.6
  34.8 3.0 copy-start.4
  34.9 178.7 %all-reduce.2.cloned.1.call-start = ((), (), s32[]{:S(2)}) async-start(), calls=%async_computation.7 | async-start | bytes 1048576 | tf_op jit(solution)/shard_map/psum | solution.py:86
  40.1 3.6 copy-start.5
  272.2 4.7 copy-start.3
  272.2 70.6 %all-to-all-start.4 = ((f32[8,352,1,256]{3,1,2,0:T(8,128)}), f32[8,352,1,256]{3,1,2,0:T(8,128)}, u32[]{:S(2)}, u32[]{:S(2)}) async-start(f32[8,352,1,256]{3,1,2,0:T(8,128)} %bitcast_dynamic-update-slice_fusion), calls=%async_computation.4 | async-start | bytes 5767168 | tf_op jit(solution)/shard_map/all_to_all | solution.py:42
  279.2 68.2 %copy-start.2 = (f32[352,2048]{0,1:T(8,128)S(1)}, f32[352,2048]{0,1:T(8,128)}, u32[]{:S(2)}) copy-start(f32[352,2048]{0,1:T(8,128)} %get-tuple-element.12) | copy-start | bytes 8650756
  342.8 70.3 %all-to-all-start = ((f32[352,8,256]{2,0,1:T(8,128)}), f32[352,8,256]{2,0,1:T(8,128)}, u32[]{:S(2)}, u32[]{:S(2)}) async-start(f32[352,8,256]{2,0,1:T(8,128)} %copy.42), calls=%async_computation | async-start | bytes 5767168 | tf_op jit(solution)/shard_map/all_to_all | solution.py:39
  349.7 67.9 %copy-start.7 = (s32[8]{0:T(128)S(1)}, s32[8]{0:T(128)}, u32[]{:S(2)}) copy-start(s32[8]{0:T(128)} %param.25) | copy-start | bytes 100
  413.1 70.3 %all-to-all-start.2 = ((f32[352,8,256]{2,0,1:T(8,128)}), f32[352,8,256]{2,0,1:T(8,128)}, u32[]{:S(2)}, u32[]{:S(2)}) async-start(f32[352,8,256]{2,0,1:T(8,128)} %copy.45), calls=%async_computation.2 | async-start | bytes 5767168 | tf_op jit(solution)/shard_map/all_to_all | solution.py:40
  561.9 70.3 %all-to-all-start.3 = ((f32[352,8,256]{2,0,1:T(8,128)}), f32[352,8,256]{2,0,1:T(8,128)}, u32[]{:S(2)}, u32[]{:S(2)}) async-start(f32[352,8,256]{2,0,1:T(8,128)} %get-tuple-element.23), calls=%async_computation.3 | async-start | bytes 5767168 | tf_op jit(solution)/shard_map/all_to_all | solution.py:35
  566.3 152.9 %all-gather.2.cloned.1.call-start = ((), (), s32[]{:S(2)}) async-start(), calls=%async_computation.8 | async-start | bytes 7208960 | tf_op jit(solution)/shard_map/all_gather | solution.py:53
  632.2 70.4 %all-to-all-start.5 = ((f32[352,8,256]{2,0,1:T(8,128)}), f32[352,8,256]{2,0,1:T(8,128)}, u32[]{:S(2)}, u32[]{:S(2)}) async-start(f32[352,8,256]{2,0,1:T(8,128)} %get-tuple-element.22), calls=%async_computation.5 | async-start | bytes 5767168 | tf_op jit(solution)/shard_map/all_to_all | solution.py:35
  719.3 6.3 copy-start.1
Sparse Core Ops, SparseCore 0:
  35.0 116.1 reduce-scatter.3
  569.0 67.8 all-gather.1
Sparse Core Ops, SparseCore 1:
  41.2 172.3 all-reduce.1
